TPU v7x, 32 devices: a whole 2x2x4 slice. The times are simulated.
32 devices in a mesh: band: 4 (over y, x), blk: 8 (over z, core).
Axes of the slice: x: 2, y: 2, z: 4, core: 2. Of those that a mesh axis runs over, the one named last changes fastest.
Arguments:
- solution: float32 [9, 2, 256, 2048], P(None, None, 'blk', 'band'), may hold values from -6 to 6
- residual: float32 [9, 2, 256, 2048], P(None, None, 'blk', 'band'), may hold values from -20 to 20
- direction: float32 [9, 2, 256, 2048], P(None, None, 'blk', 'band'), may hold values from -20 to 20
- precond: float32 [9, 2048], P(None, 'band'), may hold values from 0.2 to 2
- inv_spec: float32 [9, 2048], P(None, 'band'), may hold values from 0.05 to 2
- mixing: float32 [9, 3], replicated, may hold values from 0.1 to 2.5
- beams: float32 [9, 2048], replicated, may hold values from 0.2 to 1
- slot_band: int32 [12], replicated, may hold values from 0 to 11, each once
- m_order: int32 [256], replicated, may hold values from 0 to 255, each once
- cycle_order: int32 [128], replicated, may hold values from 0 to 127, each once
- inv_noise: float32 [12, 3, 128, 512], P('band', None, 'blk'), may hold values from 0.3 to 3
- pix_mask: int32 [128, 512], P('blk'), may hold values 0 or 1
Outputs:
- solution_next: float32 [9, 2, 256, 2048], P(None, None, 'blk', 'band')
- residual_next: float32 [9, 2, 256, 2048], P(None, None, 'blk', 'band')
- direction_next: float32 [9, 2, 256, 2048], P(None, None, 'blk', 'band')
Inputs may be any that keep to these rules, and one draw needn't show every extreme that they name: `slot_band`: slots holding a value of 9 or more are empty; each band lies in exactly one slot. `m_order`: each order 0 to 255 appears once. `cycle_order`: each cycle 0 to 127 appears once.
All inputs are finite; a program needn't handle non-finite values. No bound on the sum of `pix_mask` on one device may be relied on, other than what follows from the above.
Results may differ from a plain program's by a relative error of at most 0.0075.
Values may be sent and summed in bfloat16 or wider, within the bound.
A program may use at most 128 MiB of HBM per device.

v0:
```python
import math

import jax
import jax.numpy as jnp
from jax import lax
from jax.sharding import PartitionSpec as P

COMP = 3
STOKES = 3
FIELDS = 9
BANDS = 9
SLOTS = 3


def legendre_table(cycle_order, l_total, cycle_total):
    l_values = jnp.arange(l_total, dtype=jnp.int32)
    phase_int = l_values[None, :] * (2 * cycle_order[:, None] + 1) % (4 * cycle_total)
    angles = phase_int.astype(jnp.float32) * (math.pi / (2 * cycle_total))
    return (jnp.cos(angles) / math.sqrt(l_total)).astype(jnp.bfloat16)


def fourier_block(m_order, block_width, phi_total):
    phi_cells = jnp.arange(block_width, dtype=jnp.int32)
    phase_int = m_order[:, None] * phi_cells[None, :] % phi_total
    angles = phase_int.astype(jnp.float32) * (2.0 * math.pi / phi_total)
    scaling = 1.0 / math.sqrt(m_order.shape[0])
    return jnp.stack([jnp.cos(angles) * scaling, -jnp.sin(angles) * scaling]).astype(jnp.bfloat16)


def slot_tables(my_slots, mixing, beams):
    select = (my_slots[:, None] == jnp.arange(BANDS, dtype=jnp.int32)[None, :]).astype(jnp.float32)
    highest = lax.Precision.HIGHEST
    return (jnp.dot(select, mixing, precision=highest), jnp.dot(select, beams, precision=highest))


def band_amplitudes(rows_piece, slot_mix, slot_beam, orders):
    count = rows_piece.shape[3]
    l_values = jnp.arange(count, dtype=jnp.int32)
    triangle = (l_values[None, :] >= orders[:, None]).astype(jnp.float32)
    comp_data = rows_piece.astype(jnp.float32).reshape(COMP, STOKES, 2, orders.shape[0], count)
    mixed_sum = slot_mix[:, 0][:, None, None, None, None] * comp_data[0][None]
    for comp_index in range(1, COMP):
        mixed_sum = (
            mixed_sum
            + slot_mix[:, comp_index][:, None, None, None, None] * comp_data[comp_index][None]
        )
    return (mixed_sum * slot_beam[:, None, None, None, :] * triangle[None, None, None]).astype(
        jnp.bfloat16
    )


def sky_weights(cycle_side, m_order, weight):
    phi_total = weight.shape[3]
    block_width = phi_total // 4
    base = fourier_block(m_order, block_width, phi_total)
    turn_base = m_order % 4

    def fourier_turn(block_step, running):
        quarter = turn_base * block_step % 4
        cos_turn = jnp.where(quarter == 0, 1.0, jnp.where(quarter == 2, -1.0, 0.0)).astype(
            jnp.bfloat16
        )
        sin_turn = jnp.where(quarter == 1, 1.0, jnp.where(quarter == 3, -1.0, 0.0)).astype(
            jnp.bfloat16
        )
        real_row = base[0] * cos_turn[:, None] + base[1] * sin_turn[:, None]
        imag_row = base[1] * cos_turn[:, None] - base[0] * sin_turn[:, None]
        azim = jnp.stack([real_row, imag_row])
        sky_part = jnp.einsum(
            "sxrkm,kmp->sxrp", cycle_side, azim, preferred_element_type=jnp.float32
        )
        noise_part = lax.dynamic_slice_in_dim(weight, block_step * block_width, block_width, 3)
        weighted = (noise_part * sky_part).astype(jnp.bfloat16)
        return running + jnp.einsum(
            "sxrp,kmp->sxrkm", weighted, azim, preferred_element_type=jnp.float32
        )

    running = lax.fori_loop(0, 4, fourier_turn, jnp.zeros(cycle_side.shape, jnp.float32))
    return running.astype(jnp.bfloat16)


def combine_bands(returned, colat, slot_mix, slot_beam, orders):
    back_harm = jnp.einsum("sxrkm,rl->sxkml", returned, colat, preferred_element_type=jnp.float32)
    l_total = colat.shape[1]
    triangle = (jnp.arange(l_total, dtype=jnp.int32)[None, :] >= orders[:, None]).astype(
        jnp.float32
    )
    back_harm = back_harm * slot_beam[:, None, None, None, :] * triangle[None, None, None]
    pieces = [
        jnp.sum(slot_mix[:, comp_index][:, None, None, None, None] * back_harm, axis=0)
        for comp_index in range(COMP)
    ]
    return jnp.stack(pieces).reshape(FIELDS, 2, orders.shape[0], l_total)


def on_device(
    solution,
    residual,
    direction,
    precond,
    inv_spec,
    mixing,
    beams,
    slot_band,
    m_order,
    cycle_order,
    inv_noise,
    pix_mask,
):
    band_index = lax.axis_index("band")
    block_index = lax.axis_index("blk")
    band_count = lax.axis_size("band")
    m_local = direction.shape[2]
    l_local = direction.shape[3]
    colat = legendre_table(cycle_order, l_local * band_count, cycle_order.shape[0])
    my_orders = lax.dynamic_slice_in_dim(m_order, block_index * m_local, m_local)
    halved = direction.astype(jnp.bfloat16)
    weight = inv_noise * pix_mask.astype(jnp.float32)[None, None]
    my_slots = lax.dynamic_slice_in_dim(slot_band, band_index * SLOTS, SLOTS)
    slot_mix, slot_beam = slot_tables(my_slots, mixing, beams)
    amplitudes = band_amplitudes(
        lax.all_gather(halved, "band", axis=3, tiled=True), slot_mix, slot_beam, my_orders
    )
    colat_side = jnp.einsum(
        "sxkml,rl->sxrkm", amplitudes, colat, preferred_element_type=jnp.float32
    ).astype(jnp.bfloat16)
    cycle_side = lax.all_to_all(colat_side, "blk", split_axis=2, concat_axis=4, tiled=True)
    weighted_back = sky_weights(cycle_side, m_order, weight)
    returned = lax.all_to_all(weighted_back, "blk", split_axis=4, concat_axis=2, tiled=True)
    combined = combine_bands(returned, colat, slot_mix, slot_beam, my_orders)
    data_term = lax.psum_scatter(combined, "band", scatter_dimension=3, tiled=True)
    prior_diag = inv_spec[:, None, None, :]
    precond_full = precond[:, None, None, :]
    applied = prior_diag * direction + data_term
    scaled_res = precond_full * residual
    norm_old, curvature, crossed, squared = lax.psum(
        (
            jnp.sum(residual * scaled_res),
            jnp.sum(direction * applied),
            jnp.sum(applied * scaled_res),
            jnp.sum(applied * precond_full * applied),
        ),
        ("band", "blk"),
    )
    step_size = norm_old / curvature
    solution_next = solution + step_size * direction
    residual_next = residual - step_size * applied
    scaled_next = precond_full * residual_next
    norm_new = norm_old - 2.0 * step_size * crossed + step_size * step_size * squared
    direction_next = scaled_next + norm_new / norm_old * direction
    return (solution_next, residual_next, direction_next)


def solution(mesh):
    return jax.shard_map(
        on_device,
        mesh=mesh,
        in_specs=(
            P(None, None, "blk", "band"),
            P(None, None, "blk", "band"),
            P(None, None, "blk", "band"),
            P(None, "band"),
            P(None, "band"),
            P(),
            P(),
            P(),
            P(),
            P(),
            P("band", None, "blk", None),
            P("blk", None),
        ),
        out_specs=(
            P(None, None, "blk", "band"),
            P(None, None, "blk", "band"),
            P(None, None, "blk", "band"),
        ),
        check_vma=False,
    )
```

profile of v0, /device:TPU:0, one launch (start us, length us, event | category | flops | bytes accessed | tf_op | source)
XLA Modules:
  0.0 210.3 jit_solution(11982500947304385837)
XLA Ops:
  7.3 2.2 %convert_element_type.93 = bf16[9,2,32,512]{3,2,1,0:T(8,128)(2,1)} convert(f32[9,2,32,512]{3,2,1,0:T(8,128)} %param.16) | non-fusion elementwise | flops 294912 | bytes 1769472 | tf_op jit(solution)/shard_map/convert_element_type | solution.py:117
  9.7 0.2 fusion.47
  9.9 0.6 multiply_convert_fusion.7
  10.5 0.2 fusion.46
  10.8 39.6 %all-gather.2.cloned.1.call-done = bf16[9,2,32,2048]{3,2,1,0:T(8,128)(2,1)} async-done(((bf16[9,2,32,512]{3,2,1,0:T(8,128)(2,1)}), bf16[9,2,32,2048]{3,2,1,0:T(8,128)(2,1)}) %all-gather.2.cloned.1.call-update) | async-done | bytes 2359312 | tf_op jit(solution)/shard_map/all_gather | solution.py:122
  50.4 2.2 %fusion.61 = (f32[3,2,32,2048]{3,2,1,0:T(8,128)S(1)}, f32[3,2,32,2048]{3,2,1,0:T(8,128)S(1)}, f32[3,2,32,2048]{3,2,1,0:T(8,128)S(1)}) fusion(bf16[9,2,32,2048]{3,2,1,0:T(8,128)(2,1)} %all-gather.2.cloned.1.call-done), kind=kLoop, calls=%fused_computation.101 | loop fusion | bytes 9437184 | tf_op jit(solution)/shard_map/slice | solution.py:41
  52.6 5.2 %fusion.19 = bf16[3,3,128,2,32]{2,4,3,1,0:T(8,128)(2,1)S(1)} fusion(f32[32,2048]{1,0:T(8,128)S(1)} %fusion.39, f32[3,2048]{1,0:T(4,128)S(1)} %fusion.46, f32[3,2,32,2048]{3,2,1,0:T(8,128)S(1)} %get-tuple-element.212, f32[3]{0:T(128)S(1)} %get-tuple-element.215, f32[3,2,32,2048]{3,2,1,0:T(8,128)S(1)} %get-tuple-element.211, f32[3]{0:T(128)S(1)} %get-tuple-element.216, ...), kind=kOutput, calls=%fused_computation.45 | convolution fusion | flops 315695104 | bytes 5153316 | tf_op jit(solution)/shard_map/sxkml,rl->sxrkm/dot_general | solution.py:124
  57.8 0.6 copy.24
  58.5 1.1 reshape.220
  59.6 4.6 %all-to-all-start = ((bf16[8,2,4608]{2,1,0:T(2,128)(2,1)}), bf16[8,2,4608]{2,1,0:T(2,128)(2,1)S(1)}, u32[]{:S(2)}, u32[]{:S(2)}) async-start(bf16[8,2,4608]{2,1,0:T(2,128)(2,1)} %reshape.220), calls=%async_computation | async-start | bytes 294912 | tf_op jit(solution)/shard_map/all_to_all | solution.py:127
  64.3 6.8 %all-to-all-done = bf16[8,2,4608]{2,1,0:T(2,128)(2,1)S(1)} async-done(((bf16[8,2,4608]{2,1,0:T(2,128)(2,1)}), bf16[8,2,4608]{2,1,0:T(2,128)(2,1)S(1)}, u32[]{:S(2)}, u32[]{:S(2)}) %all-to-all-start) | async-done | bytes 147488 | tf_op jit(solution)/shard_map/all_to_all | solution.py:127
  71.2 0.3 reshape.221
  71.6 0.2 copy.26
  71.8 0.4 all_to_all.29
  72.1 2.5 %while.16 = (s32[]{:T(128)}, f32[3,3,16,2,256]{4,2,3,1,0:T(8,128)S(1)}, f32[3,3,16,512]{3,2,1,0:T(8,128)S(1)}, bf16[2,256,128]{2,1,0:T(8,128)(2,1)S(1)}, s32[256...) while((s32[]{:T(128)}, ...), condition=%wide.region_3.4_spmd.clone, body=%wide.region_2.3_spmd.clone.sunk | while | flops 38659592 | bytes 1340589 | solution.py:78
  72.2 0.1 multiply_add_fusion.7
  72.3 0.4 convolution_add_fusion.2
  72.8 0.1 multiply_add_fusion.7
  73.0 0.4 convolution_add_fusion.2
  73.6 0.4 convolution_add_fusion.2
  74.2 0.4 convolution_add_fusion.2
  74.7 1.2 copy.27
  75.9 1.2 reshape.222
  77.2 9.6 %all_to_all.36 = bf16[8,2,4608]{2,1,0:T(2,128)(2,1)S(1)} all-to-all(bf16[8,2,4608]{2,1,0:T(2,128)(2,1)S(1)} %reshape.222), channel_id=1, replica_groups=mesh['band'=4,'blk'=8] {'blk'}, dimensions={0} | all-to-all | bytes 294912 | tf_op jit(solution)/shard_map/all_to_all | solution.py:129
  86.8 0.8 reshape.223
  87.6 0.9 copy.28
  88.5 6.0 %multiply_reduce_fusion.2 = (f32[3,2,32,2048]{3,2,1,0:T(8,128)S(1)}, f32[3,2,32,2048]{3,2,1,0:T(8,128)S(1)}, f32[3,2,32,2048]{3,2,1,0:T(8,128)S(1)}) fusion(f32[32,2048]{1,0:T(8,128)S(1)} %fusion.39, f32[3,2048]{1,0:T(4,128)S(1)} %fusion.46, f32[3]{0:T(128)S(1)} %get-tuple-element.214, f32[3]{0:T(128)S(1)} %get-tuple-element.216, ...), kind=kOutput, calls=%fused_computation.26 | convolution fusion | flops 314441728 | bytes 5153316 | tf_op jit(solution)/shard_map/sxrkm,rl->sxkml/dot_general | solution.py:83
  94.5 2.7 %pad_maximum_fusion = f32[3,3,2,32,2048]{4,3,2,1,0:T(8,128)} fusion(f32[1,3,2,32,2048]{4,3,2,1,0:T(8,128)S(1)} %bitcast.82, f32[1,3,2,32,2048]{4,3,2,1,0:T(8,128)S(1)} %bitcast.81, f32[1,3,2,32,2048]{4,3,2,1,0:T(8,128)S(1)} %bitcast.80), kind=kLoop, calls=%fused_computation.23 | loop fusion | flops 2359296 | bytes 9437184 | tf_op jit(solution)/shard_map/stack | solution.py:93
  97.2 55.4 %reduce-scatter.2.cloned.1.call-done = f32[9,2,32,512]{3,2,1,0:T(8,128)} async-done(((f32[9,2,32,2048]{3,2,1,0:T(8,128)}), f32[9,2,32,512]{3,2,1,0:T(8,128)}) %reduce-scatter.2.cloned.1.call-update) | async-done | bytes 1179664 | tf_op jit(solution)/shard_map/reduce_scatter | solution.py:131
  152.6 3.5 %fusion.17 = (f32[]{:T(128)}, f32[]{:T(128)}, f32[]{:T(128)}, f32[]{:T(128)}, f32[9,2,32,512]{3,2,1,0:T(8,128)}) fusion(f32[9,512]{1,0:T(8,128)S(1)} %copy-done.4, f32[9,2,32,512]{3,2,1,0:T(8,128)S(1)} %copy-done.2, f32[9,2,32,512]{3,2,1,0:T(8,128)S(1)} %copy-done.1, f32[9,2,32,512]{3,2,1,0:T(8,128)} %reduce-scatter.2.cloned.1.call-done, ...), kind=kLoop, calls=%fused_computation.38 | loop fusion | flops 3538940 | bytes 4755472 | tf_op jit(solution)/shard_map/reduce_sum | solution.py:141
  156.1 39.7 %all-reduce = (f32[]{:T(128)}, f32[]{:T(128)}, f32[]{:T(128)}, f32[]{:T(128)}) all-reduce(f32[]{:T(128)} %get-tuple-element.185, f32[]{:T(128)} %get-tuple-element.186, f32[]{:T(128)} %get-tuple-element.184, f32[]{:T(128)} %get-tuple-element.183), channel_id=1, replica_groups=mesh['band'=4,'blk'=8] {'band','blk'}, use_global_device_ids=true, to_apply=%region_1.2 | all-reduce | flops 4 | bytes 32 | tf_op jit(solution)/shard_map/psum | solution.py:136
  199.5 3.9 %multiply_add_fusion.1 = (f32[9,2,32,512]{3,2,1,0:T(8,128)}, f32[9,2,32,512]{3,2,1,0:T(8,128)}, f32[9,2,32,512]{3,2,1,0:T(8,128)}) fusion(f32[9,2,32,512]{3,2,1,0:T(8,128)S(1)} %copy-done.1, f32[]{:T(128)S(6)} %div.15, f32[9,512]{1,0:T(8,128)S(1)} %copy-done.4, f32[9,2,32,512]{3,2,1,0:T(8,128)S(1)} %copy-done.2, f32[9,2,32,512]{3,2,1,0:T(8,128)} %get-tuple-element.207, ...), kind=kLoop, calls=%fused_computation.39 | loop fusion | flops 2064384 | bytes 8275976 | tf_op jit(solution)/shard_map/add | solution.py:150
  (48 shorter events, 0.9 us)
Async XLA Ops:
  7.2 3.3 %copy-start = (f32[9,2048]{1,0:T(8,128)S(1)}, f32[9,2048]{1,0:T(8,128)}, u32[]{:S(2)}) copy-start(f32[9,2048]{1,0:T(8,128)} %param.20) | copy-start | bytes 221188
  7.2 2.3 %copy-start.7 = (s32[256]{0:T(256)S(1)}, s32[256]{0:T(256)}, u32[]{:S(2)}) copy-start(s32[256]{0:T(256)} %param.22) | copy-start | bytes 3076
  7.2 2.4 %copy-start.9 = (s32[12]{0:T(128)S(1)}, s32[12]{0:T(128)}, u32[]{:S(2)}) copy-start(s32[12]{0:T(128)} %param.21) | copy-start | bytes 148
  7.2 2.5 %copy-start.10 = (s32[128]{0:T(128)S(1)}, s32[128]{0:T(128)}, u32[]{:S(2)}) copy-start(s32[128]{0:T(128)} %param.23) | copy-start | bytes 1540
  7.2 2.5 %copy-start.8 = (f32[9,3]{0,1:T(4,128)S(1)}, f32[9,3]{0,1:T(4,128)}, u32[]{:S(2)}) copy-start(f32[9,3]{0,1:T(4,128)} %param.19) | copy-start | bytes 328
  7.2 43.2 %all-gather.2.cloned.1.call-start = ((), (), s32[]{:S(2)}) async-start(), calls=%async_computation.3 | async-start | bytes 2949120 | tf_op jit(solution)/shard_map/all_gather | solution.py:122
  57.8 6.5 %copy-start.6 = (s32[16,512]{1,0:T(8,128)S(1)}, s32[16,512]{1,0:T(8,128)}, u32[]{:S(2)}) copy-start(s32[16,512]{1,0:T(8,128)} %param.25) | copy-start | bytes 98308
  57.8 6.5 %copy-start.3 = (f32[3,3,16,512]{3,2,1,0:T(8,128)S(1)}, f32[3,3,16,512]{3,2,1,0:T(8,128)}, u32[]{:S(2)}) copy-start(f32[3,3,16,512]{3,2,1,0:T(8,128)} %param.24) | copy-start | bytes 884740
  59.6 11.6 %all-to-all-start = ((bf16[8,2,4608]{2,1,0:T(2,128)(2,1)}), bf16[8,2,4608]{2,1,0:T(2,128)(2,1)S(1)}, u32[]{:S(2)}, u32[]{:S(2)}) async-start(bf16[8,2,4608]{2,1,0:T(2,128)(2,1)} %reshape.220), calls=%async_computation | async-start | bytes 294912 | tf_op jit(solution)/shard_map/all_to_all | solution.py:127
  64.2 88.4 %reduce-scatter.2.cloned.1.call-start = ((), (), s32[]{:S(2)}) async-start(), calls=%async_computation.4 | async-start | bytes 5898240 | tf_op jit(solution)/shard_map/reduce_scatter | solution.py:131
  97.2 55.4 %copy-start.1 = (f32[9,2,32,512]{3,2,1,0:T(8,128)S(1)}, f32[9,2,32,512]{3,2,1,0:T(8,128)}, u32[]{:S(2)}) copy-start(f32[9,2,32,512]{3,2,1,0:T(8,128)} %param.16) | copy-start | bytes 3538948
  97.2 55.4 %copy-start.2 = (f32[9,2,32,512]{3,2,1,0:T(8,128)S(1)}, f32[9,2,32,512]{3,2,1,0:T(8,128)}, u32[]{:S(2)}) copy-start(f32[9,2,32,512]{3,2,1,0:T(8,128)} %param.15) | copy-start | bytes 3538948
  97.2 55.4 %copy-start.4 = (f32[9,512]{1,0:T(8,128)S(1)}, f32[9,512]{1,0:T(8,128)}, u32[]{:S(2)}) copy-start(f32[9,512]{1,0:T(8,128)} %param.17) | copy-start | bytes 55300
  97.2 55.4 %copy-start.5 = (f32[9,512]{1,0:T(8,128)S(1)}, f32[9,512]{1,0:T(8,128)}, u32[]{:S(2)}) copy-start(f32[9,512]{1,0:T(8,128)} %param.18) | copy-start | bytes 55300
Sparse Core Ops, SparseCore 0:
  10.4 39.9 all-gather.1
  97.3 55.2 reduce-scatter.1
where the time goes:
time: 211 us; the launch traced here: 210 us
  waiting for transfers between devices  102 us (48%)
  blocking collectives  49.3 us (23%)
  between operations  18.1 us (9%)
  other arithmetic  13.7 us (6%)
  matrix products  13.3 us (6%)
  local copies, waits for them, and re-layouts  9.24 us (4%)
  starting transfers between devices  4.68 us (2%)
    reduce_scatter x1, waiting for transfers between devices, on_device(): lax.psum_scatter(combined, 'band', scatter_dimension=3, tiled=True)  55.4 us
    psum x1, blocking collectives, on_device(): lax.psum((jnp.sum(residual * scaled_res), jnp.sum(direction * applied), j...  39.7 us
    all_gather x1, waiting for transfers between devices, on_device(): lax.all_gather(halved, 'band', axis=3, tiled=True)  39.6 us
    all_to_all x1, blocking collectives, on_device(): lax.all_to_all(weighted_back, 'blk', split_axis=4, concat_axis=2, tiled=T...  9.62 us
    all_to_all x1, waiting for transfers between devices, on_device(): lax.all_to_all(colat_side, 'blk', split_axis=2, concat_axis=4, tiled=True)  6.82 us
    dot_general x1, matrix products, combine_bands(): jnp.einsum('sxrkm,rl->sxkml', returned, colat, preferred_element_type=jnp...  5.99 us
    dot_general x1, matrix products, on_device(): jnp.einsum('sxkml,rl->sxrkm', amplitudes, colat, preferred_element_type=j...  5.19 us
    all_to_all x1, starting transfers between devices, on_device(): lax.all_to_all(colat_side, 'blk', split_axis=2, concat_axis=4, tiled=True)  4.61 us
  transfers between devices with their start and end apart: 3, of which 3 were waited for; matrix products, arithmetic and copies ran while one was open for 1% of the time, Pallas kernels for 0%

commit v1 on v0

v1 whole, which is shorter than its diff:
```python
import functools
import math

import jax
import jax.numpy as jnp
from jax import lax
from jax.experimental import pallas as pl
from jax.experimental.pallas import tpu as pltpu
from jax.sharding import PartitionSpec as P

COMP = 3
STOKES = 3
FIELDS = 9
BANDS = 9
LANES = 512
MESH = pl.DeviceIdType.MESH


def wave(phase, quarter):
    folded = jnp.abs(phase - 2 * quarter) - quarter
    x = folded.astype(jnp.float32) * (math.pi / (2 * quarter))
    x2 = x * x
    series = -1.0 / 39916800.0
    for coefficient in (1.0 / 362880.0, -1.0 / 5040.0, 1.0 / 120.0, -1.0 / 6.0, 1.0):
        series = series * x2 + coefficient
    return x * series


def wrapped(value, period):
    if period & (period - 1) == 0:
        return value & (period - 1)
    return lax.rem(value, period)


def contract(left, right, left_dim, right_dim):
    return lax.dot_general(
        left, right, (((left_dim,), (right_dim,)), ((), ())), preferred_element_type=jnp.float32
    )


def wait_bytes(ref, sem):
    pltpu.make_async_copy(ref, ref, sem).wait()


def kernel(
    sizes,
    direction,
    residual,
    precond,
    inv_spec,
    slot_mix,
    slot_beam,
    my_orders,
    all_orders,
    cycles,
    noise,
    mask,
    applied,
    totals,
    tri,
    halved,
    colat,
    amps,
    send,
    recv,
    azim,
    side,
    back,
    back_send,
    back_recv,
    stats,
    send_sem,
    recv_sem,
    back_send_sem,
    back_recv_sem,
    stat_send_sem,
    stat_recv_sem,
):
    groups, blocks, slots, l_total, modes, phi_total = sizes
    rows, l_local = direction.shape[1:]
    cycle_total = cycles.shape[0]
    r_local = cycle_total // blocks
    pairs = slots * STOKES
    per_lane = 128 // rows
    my_band = lax.axis_index("band")
    my_block = lax.axis_index("blk")

    def target(step, shift):
        return (lax.rem(my_band + step, groups), lax.rem(my_block + shift, blocks))

    barrier = pltpu.get_barrier_semaphore()

    def greet(flat, carry):
        pl.semaphore_signal(
            barrier, inc=1, device_id=target(flat // blocks, flat % blocks), device_id_type=MESH
        )
        return carry

    lax.fori_loop(1, groups * blocks, greet, 0)

    l_index = my_band * l_local + lax.broadcasted_iota(jnp.int32, (1, l_local), 1)
    tri[...] = jnp.where(l_index >= my_orders[...], 1.0, 0.0)
    for field in range(FIELDS):
        halved[field] = direction[field].astype(jnp.bfloat16).astype(jnp.float32) * tri[...]

    def colat_rows(at, carry):
        at_rows = pl.ds(pl.multiple_of(at * 64, 64), 64)
        phase = wrapped(l_index * (2 * cycles[at_rows, :] + 1), 4 * cycle_total)
        colat[at_rows, :] = (wave(phase, cycle_total) / math.sqrt(l_total)).astype(jnp.bfloat16)
        return carry

    lax.fori_loop(0, cycle_total // 64, colat_rows, 0)

    def transform(step):
        group = lax.rem(my_band + step, groups)
        for slot in range(slots):
            at = group * slots + slot
            beam = slot_beam[at]
            for stokes in range(STOKES):
                mixed = slot_mix[at * COMP] * halved[stokes]
                for comp in range(1, COMP):
                    mixed = mixed + slot_mix[at * COMP + comp] * halved[comp * STOKES + stokes]
                first = (slot * STOKES + stokes) * rows
                amps[first : first + rows, :] = (mixed * beam).astype(jnp.bfloat16)
        send[step] = contract(colat[...], amps[...], 1, 1).astype(jnp.bfloat16)

    def block_rows(block):
        return pl.ds(pl.multiple_of(block * r_local, r_local), r_local)

    def ship(step, shift):
        there = target(step, shift)
        pltpu.make_async_remote_copy(
            src_ref=send.at[step, block_rows(there[1])],
            dst_ref=recv.at[step, block_rows(shift)],
            send_sem=send_sem.at[step],
            recv_sem=recv_sem.at[step],
            device_id=there,
            device_id_type=MESH,
        ).start()

    def ship_from(step, first):
        def one(shift, carry):
            ship(step, shift)
            return carry

        lax.fori_loop(first, blocks, one, 0)

    transform(1)
    pl.semaphore_wait(barrier, groups * blocks - 1)
    ship_from(1, 0)

    def group_step(step, carry):
        transform(step)
        ship_from(step, 0)
        return carry

    lax.fori_loop(2, groups, group_step, 0)
    transform(0)
    ship_from(0, 1)
    recv[0, 0:r_local] = send[0, block_rows(my_block)]

    def fill_azim(chunk):
        cell = chunk * LANES + lax.broadcasted_iota(jnp.int32, (1, LANES), 1)

        def one(at, carry):
            at_rows = pl.ds(pl.multiple_of(at * 2 * rows, 2 * rows), 2 * rows)
            turned = lax.broadcasted_iota(jnp.int32, (2 * rows, 1), 0) % rows >= rows // 2
            shift = jnp.where(turned, phi_total // 4, 0)
            phase = wrapped(all_orders[at_rows, :] * cell + shift, phi_total)
            azim[at_rows, :] = (wave(phase, phi_total // 4) / math.sqrt(modes)).astype(jnp.bfloat16)
            return carry

        lax.fori_loop(0, blocks // 2, one, 0)

    chunks = phi_total // LANES
    if chunks == 1:
        fill_azim(0)
    residual_sum = jnp.zeros((rows, l_local), jnp.float32)
    for field in range(FIELDS):
        residual_sum = residual_sum + residual[field] * (precond[field] * residual[field])

    rest = (blocks - 1) * r_local
    wait_bytes(recv.at[0, 0:rest], recv_sem.at[0])
    wait_bytes(recv.at[1], recv_sem.at[1])
    for step in range(2, groups):
        wait_bytes(recv.at[step], recv_sem.at[step])

    def gather(at, carry):
        parts = []
        for inner in range(per_lane):
            block = at * per_lane + inner
            rows_at = block_rows(lax.rem(my_block - block + blocks, blocks))
            total = recv[0, rows_at, :].astype(jnp.float32)
            for step in range(1, groups):
                total = total + recv[step, rows_at, :].astype(jnp.float32)
            parts.append(total)
        columns = pl.ds(pl.multiple_of(at * 128, 128), 128)
        for pair in range(pairs):
            picked = [part[:, pair * rows : (pair + 1) * rows] for part in parts]
            joined = jnp.concatenate(picked, axis=1).astype(jnp.bfloat16)
            side[pair * r_local : (pair + 1) * r_local, columns] = joined
        return carry

    lax.fori_loop(0, blocks // per_lane, gather, 0)

    def weigh(chunk):
        columns = pl.ds(pl.multiple_of(chunk * LANES, LANES), LANES)
        sky = contract(side[...], azim[...], 1, 0).reshape(pairs, r_local, LANES)
        weight = noise[:, :, columns] * mask[:, columns].astype(jnp.float32)[None]
        weighted = (weight * sky).astype(jnp.bfloat16).reshape(pairs * r_local, LANES)
        return contract(weighted, azim[...], 1, 1)

    if chunks == 1:
        back[...] = weigh(0)
    else:
        back[...] = jnp.zeros_like(back)

        def one_chunk(chunk, carry):
            fill_azim(chunk)
            back[...] += weigh(chunk)
            return carry

        lax.fori_loop(0, chunks, one_chunk, 0)

    def scatter(at, carry):
        columns = pl.ds(pl.multiple_of(at * 128, 128), 128)
        wide = [back[pair * r_local : (pair + 1) * r_local, columns] for pair in range(pairs)]
        for inner in range(per_lane):
            picked = [part[:, inner * rows : (inner + 1) * rows] for part in wide]
            joined = jnp.concatenate(picked, axis=1).astype(jnp.bfloat16)
            back_send[at * per_lane + inner] = joined
        return carry

    lax.fori_loop(0, blocks // per_lane, scatter, 0)

    def return_to(step, shift):
        there = target(step, shift)
        pltpu.make_async_remote_copy(
            src_ref=back_send.at[there[1]],
            dst_ref=back_recv.at[step, block_rows(my_block)],
            send_sem=back_send_sem.at[step],
            recv_sem=back_recv_sem.at[step],
            device_id=there,
            device_id_type=MESH,
        ).start()

    def return_step(step, first):
        def one(shift, carry):
            return_to(step, shift)
            return carry

        lax.fori_loop(first, blocks, one, 0)

    return_step(0, 1)
    for step in range(1, groups):
        return_step(step, 0)
    back_recv[0, block_rows(my_block)] = back_send[my_block]
    applied[...] = jnp.zeros_like(applied)

    def combine(step):
        group = lax.rem(my_band - step + groups, groups)
        harm = contract(back_recv[step], colat[...], 0, 0)
        for stokes in range(STOKES):
            sums = [applied[comp * STOKES + stokes] for comp in range(COMP)]
            for slot in range(slots):
                at = group * slots + slot
                first = (slot * STOKES + stokes) * rows
                term = harm[first : first + rows, :] * slot_beam[at]
                sums = [sums[comp] + slot_mix[at * COMP + comp] * term for comp in range(COMP)]
            for comp in range(COMP):
                applied[comp * STOKES + stokes] = sums[comp]

    wait_bytes(back_recv.at[0, 0:rest], back_recv_sem.at[0])
    combine(0)

    def combine_step(step, carry):
        wait_bytes(back_recv.at[step], back_recv_sem.at[step])
        combine(step)
        return carry

    lax.fori_loop(1, groups, combine_step, 0)

    curvature = jnp.zeros((rows, l_local), jnp.float32)
    crossed = jnp.zeros((rows, l_local), jnp.float32)
    squared = jnp.zeros((rows, l_local), jnp.float32)
    for field in range(FIELDS):
        held = direction[field]
        value = inv_spec[field] * held + applied[field] * tri[...]
        applied[field] = value
        scaled = precond[field] * value
        curvature = curvature + held * value
        crossed = crossed + residual[field] * scaled
        squared = squared + value * scaled

    def lane_sums(value):
        row = jnp.sum(value, axis=0, keepdims=True)
        return functools.reduce(
            jnp.add, [row[:, at : at + 128] for at in range(0, l_local, 128)]
        )

    stats[0] = jnp.concatenate(
        [lane_sums(v) for v in (residual_sum, curvature, crossed, squared)]
        + [jnp.zeros((4, 128), jnp.float32)],
        axis=0,
    )

    def tell(flat, carry):
        pltpu.make_async_remote_copy(
            src_ref=stats.at[0],
            dst_ref=stats.at[flat],
            send_sem=stat_send_sem,
            recv_sem=stat_recv_sem,
            device_id=target(flat // blocks, flat % blocks),
            device_id_type=MESH,
        ).start()
        return carry

    lax.fori_loop(1, groups * blocks, tell, 0)
    wait_bytes(stats.at[1 : groups * blocks], stat_recv_sem)
    summed = jnp.sum(jnp.sum(stats[...], axis=0), axis=1, keepdims=True)
    totals[...] = jnp.broadcast_to(summed, totals.shape)

    wait_bytes(stats.at[1 : groups * blocks], stat_send_sem)
    wait_bytes(recv.at[0, 0:rest], send_sem.at[0])
    wait_bytes(back_recv.at[0, 0:rest], back_send_sem.at[0])
    for step in range(1, groups):
        wait_bytes(recv.at[step], send_sem.at[step])
        wait_bytes(back_recv.at[step], back_send_sem.at[step])


def on_device(
    solution,
    residual,
    direction,
    precond,
    inv_spec,
    mixing,
    beams,
    slot_band,
    m_order,
    cycle_order,
    inv_noise,
    pix_mask,
):
    band_index = lax.axis_index("band")
    block_index = lax.axis_index("blk")
    groups = lax.axis_size("band")
    blocks = lax.axis_size("blk")
    m_local, l_local = direction.shape[2:]
    rows = 2 * m_local
    modes = m_order.shape[0]
    cycle_total = cycle_order.shape[0]
    slots, _, r_local, phi_total = inv_noise.shape
    pairs = slots * STOKES
    devices = groups * blocks

    select = (slot_band[:, None] == jnp.arange(BANDS, dtype=jnp.int32)[None, :]).astype(jnp.float32)
    slot_mix = jnp.sum(select[:, :, None] * mixing[None], axis=1).reshape(-1)
    my_beams = lax.dynamic_slice_in_dim(beams, band_index * l_local, l_local, 1)
    slot_beam = jnp.sum(select[:, :, None] * my_beams[None], axis=1)[:, None, :]
    by_block = m_order.reshape(blocks, m_local)
    all_orders = jnp.concatenate([by_block, by_block], axis=1)
    my_orders = lax.dynamic_slice_in_dim(all_orders, block_index, 1).reshape(rows, 1)

    vmem = pl.BlockSpec(memory_space=pltpu.VMEM)
    smem = pl.BlockSpec(memory_space=pltpu.SMEM)
    bf16, f32 = jnp.bfloat16, jnp.float32
    field_shape = (FIELDS, rows, l_local)
    dma = pltpu.SemaphoreType.DMA
    sizes = (groups, blocks, slots, l_local * groups, modes, phi_total)
    applied, totals = pl.pallas_call(
        functools.partial(kernel, sizes),
        out_shape=(
            jax.ShapeDtypeStruct(field_shape, f32),
            jax.ShapeDtypeStruct((8, 128), f32),
        ),
        in_specs=[vmem] * 4 + [smem] + [vmem] * 6,
        out_specs=(vmem, vmem),
        scratch_shapes=[
            pltpu.VMEM((rows, l_local), f32),
            pltpu.VMEM(field_shape, f32),
            pltpu.VMEM((cycle_total, l_local), bf16),
            pltpu.VMEM((pairs * rows, l_local), bf16),
            pltpu.VMEM((groups, cycle_total, pairs * rows), bf16),
            pltpu.VMEM((groups, cycle_total, pairs * rows), bf16),
            pltpu.VMEM((blocks * rows, LANES), bf16),
            pltpu.VMEM((pairs * r_local, blocks * rows), bf16),
            pltpu.VMEM((pairs * r_local, blocks * rows), f32),
            pltpu.VMEM((blocks, r_local, pairs * rows), bf16),
            pltpu.VMEM((groups, cycle_total, pairs * rows), bf16),
            pltpu.VMEM((devices, 8, 128), f32),
            dma((groups,)),
            dma((groups,)),
            dma((groups,)),
            dma((groups,)),
            dma,
            dma,
        ],
        compiler_params=pltpu.CompilerParams(
            collective_id=0, has_side_effects=True, vmem_limit_bytes=60 * 1024 * 1024
        ),
    )(
        direction.reshape(field_shape),
        residual.reshape(field_shape),
        precond[:, None, :],
        inv_spec[:, None, :],
        slot_mix,
        slot_beam,
        my_orders,
        all_orders.reshape(blocks * rows, 1),
        cycle_order[:, None],
        inv_noise.reshape(pairs, r_local, phi_total),
        pix_mask,
    )
    applied = applied.reshape(direction.shape)
    norm_old, curvature, crossed, squared = (totals[at, 0] for at in range(4))
    precond_full = precond[:, None, None, :]
    step_size = norm_old / curvature
    solution_next = solution + step_size * direction
    residual_next = residual - step_size * applied
    norm_new = norm_old - 2.0 * step_size * crossed + step_size * step_size * squared
    direction_next = precond_full * residual_next + norm_new / norm_old * direction
    return (solution_next, residual_next, direction_next)


def solution(mesh):
    field = P(None, None, "blk", "band")
    return jax.shard_map(
        on_device,
        mesh=mesh,
        in_specs=(
            field,
            field,
            field,
            P(None, "band"),
            P(None, "band"),
            P(),
            P(),
            P(),
            P(),
            P(),
            P("band", None, "blk", None),
            P("blk", None),
        ),
        out_specs=(field, field, field),
        check_vma=False,
    )
```

time: 211 us -> 69.9 us (0.33)
  waiting for transfers between devices: 102 us -> 0 us
  Pallas kernels: 0 us -> 49.7 us
  blocking collectives: 49.3 us -> 0 us
  between operations: 18.1 us -> 4.65 us
  matrix products: 13.3 us -> 0 us
  other arithmetic: 13.7 us -> 4.77 us
  starting transfers between devices: 4.68 us -> 0 us
    reduce_scatter x1 -> x0, waiting for transfers between devices: 55.4 us -> none  [on_device(): lax.psum_scatter(combined, 'band', scatter_dimension=3, tiled=True)]
    pallas_call x0 -> x1, Pallas kernels: none -> 49.7 us  [on_device(): pl.pallas_call(functools.partial(kernel, sizes), out_shape=(jax.ShapeDtyp...]
    psum x1 -> x0, blocking collectives: 39.7 us -> none  [on_device(): lax.psum((jnp.sum(residual * scaled_res), jnp.sum(direction * applied), j...]
    all_gather x1 -> x0, waiting for transfers between devices: 39.6 us -> none  [on_device(): lax.all_gather(halved, 'band', axis=3, tiled=True)]
    dot_general x8 -> x0, matrix products: 13.3 us -> none  [the longest x1 5.99 us: combine_bands(): jnp.einsum('sxrkm,rl->sxkml', returned, colat, preferred_element_type=jnp...]
    all_to_all x1 -> x0, blocking collectives: 9.62 us -> none  [on_device(): lax.all_to_all(weighted_back, 'blk', split_axis=4, concat_axis=2, tiled=T...]
    all_to_all x1 -> x0, waiting for transfers between devices: 6.82 us -> none  [on_device(): lax.all_to_all(colat_side, 'blk', split_axis=2, concat_axis=4, tiled=True)]
    broadcast_in_dim x0 -> x4, local copies, waits for them, and re-layouts: none -> 4.76 us  [the longest x1 1.39 us: on_device(): cycle_order[:, None]]
  transfers between devices with their start and end apart: 3 -> 0, of which waited for: 3 -> 0; matrix products, arithmetic and copies ran while one was open for 1% -> 0% of each run, Pallas kernels for 0% -> 0%
where the time goes in v1:
time: 69.9 us; the launch traced here: 69.5 us
  Pallas kernels  49.7 us (71%)
  local copies, waits for them, and re-layouts  10.4 us (15%)
  other arithmetic  4.77 us (7%)
  between operations  4.65 us (7%)
    pallas_call x1, Pallas kernels, on_device(): pl.pallas_call(functools.partial(kernel, sizes), out_shape=(jax.ShapeDtyp...  49.7 us
    add x1, other arithmetic, on_device(): precond_full * residual_next + norm_new / norm_old * direction  2.28 us
    mul x1, other arithmetic, on_device(): residual_next = residual - step_size * applied  1.58 us

profile of v1, /device:TPU:0, one launch (start us, length us, event | category | flops | bytes accessed | tf_op | source)
XLA Modules:
  0.0 69.5 jit_solution(12903064632467881134)
XLA Ops:
  0.6 0.0 copy-start
  0.7 0.8 %reshape.58 = s32[8,32]{1,0:T(8,128)S(1)} reshape(s32[256]{0:T(256)} %param.20) | data formatting | bytes 2048 | tf_op jit(solution)/shard_map/reshape | solution.py:361
  1.4 0.1 pad_add_fusion
  1.5 0.7 fusion
  2.2 0.8 %copy.22 = f32[9,3]{1,0:T(8,128)S(1)} copy(f32[9,3]{0,1:T(4,128)} %param.17) | data formatting | bytes 216 | tf_op args[5]
  3.0 0.1 multiply_reduce_fusion.1
  3.0 0.1 copy.23
  3.1 0.7 reshape.57.slot_mix
  3.8 1.4 %broadcast_in_dim.9.inv_spec = f32[9,1,512]{2,1,0:T(1,128)} reshape(f32[9,512]{1,0:T(8,128)} %param.16) | data formatting | bytes 36864 | tf_op jit(solution)/shard_map/broadcast_in_dim | solution.py:406
  5.2 1.4 %broadcast_in_dim.8.precond = f32[9,1,512]{2,1,0:T(1,128)} reshape(f32[9,512]{1,0:T(8,128)} %param.15) | data formatting | bytes 36864 | tf_op jit(solution)/shard_map/broadcast_in_dim | solution.py:405
  6.5 0.7 %copy.24.my_orders = s32[64,1]{1,0:T(8,128)} copy(s32[64,1]{0,1:T(1,128)S(1)} %dynamic-slice_bitcast_fusion) | data formatting | bytes 512 | tf_op jit(solution)/shard_map/reshape | solution.py:363
  7.3 0.0 copy-done
  7.3 0.1 multiply_reduce_fusion
  7.4 0.6 broadcast_in_dim.10.slot_beam
  8.0 1.4 %copy.26.cycles = s32[128,1]{1,0:T(8,128)} copy(s32[128,1]{0,1:T(1,128)} %bitcast.15) | data formatting | bytes 1024 | tf_op jit(solution)/shard_map/broadcast_in_dim | solution.py:411
  9.4 0.9 %reshape.62.all_orders = s32[512,1]{1,0:T(8,128)} reshape(s32[8,64]{1,0:T(8,128)S(1)} %pad_add_fusion) | data formatting | bytes 4096 | tf_op jit(solution)/shard_map/reshape | solution.py:410
  10.3 0.0 copy-start.3
  10.3 0.0 copy-start.4
  10.3 49.7 %shard_map.139 = (f32[9,64,512]{2,1,0:T(8,128)}, f32[8,128]{1,0:T(8,128)}) custom-call(f32[9,64,512]{2,1,0:T(8,128)} %bitcast.12, f32[9,64,512]{2,1,0:T(8,128)} %bitcast.13, f32[9,1,512]{2,1,0:T(1,128)} %broadcast_in_dim.8.precond, f32[9,1,512]{2,1,0:T(1,128)} %broadcast_in_dim.9.inv_spec, f32[36]{0:T(128)} %reshape.57.slot_mix, ...), custom_call_target="tpu_custom_call" | custom-call | tf_op jit(solution)/shard_map/pallas_call | solution.py:371
  60.0 1.4 %fusion.1 = (f32[1,1]{1,0:T(1,128)}, f32[1,1]{1,0:T(1,128)}, f32[1,1]{1,0:T(1,128)}, f32[1,1]{1,0:T(1,128)}) fusion(f32[8,128]{1,0:T(8,128)} %get-tuple-element.5), kind=kLoop, calls=%fused_computation.10 | loop fusion | bytes 32 | tf_op jit(solution)/shard_map/slice | solution.py:416
  65.2 0.0 copy-start.1
  65.3 0.0 copy-start.2
  65.3 1.6 %broadcast_multiply_fusion = f32[9,64,512]{2,1,0:T(8,128)S(1)} fusion(f32[9,64,512]{2,1,0:T(8,128)} %get-tuple-element.6, f32[]{:T(128)S(6)} %div.6), kind=kLoop, calls=%fused_computation.2 | loop fusion | flops 294912 | bytes 2359300 | tf_op jit(solution)/shard_map/mul | solution.py:420
  66.9 0.0 copy-done.3
  66.9 0.0 copy-done.4
  66.9 0.0 copy-done.1
  66.9 0.3 copy-done.2
  67.2 2.3 %multiply_add_fusion = (f32[9,2,32,512]{3,2,1,0:T(8,128)}, f32[9,2,32,512]{3,2,1,0:T(8,128)}, f32[9,2,32,512]{3,2,1,0:T(8,128)}) fusion(f32[9,2,32,512]{3,2,1,0:T(8,128)S(1)} %copy-done.1, f32[]{:T(128)S(6)} %div.7, f32[9,512]{1,0:T(8,128)S(1)} %copy-done.4, f32[9,2,32,512]{3,2,1,0:T(8,128)S(1)} %copy-done.2, f32[9,2,32,512]{3,2,1,0:T(8,128)S(1)} %bitcast.11, ...), kind=kLoop, calls=%fused_computation | loop fusion | flops 1769472 | bytes 8275976 | tf_op jit(solution)/shard_map/add | solution.py:422
  (2 shorter events, 0.0 us)
Async XLA Ops:
  0.6 6.6 %copy-start = (f32[9,2048]{1,0:T(8,128)S(1)}, f32[9,2048]{1,0:T(8,128)}, u32[]{:S(2)}) copy-start(f32[9,2048]{1,0:T(8,128)} %param.18) | copy-start | bytes 221188
  10.3 56.6 %copy-start.3 = (f32[9,2,32,512]{3,2,1,0:T(8,128)S(1)}, f32[9,2,32,512]{3,2,1,0:T(8,128)}, u32[]{:S(2)}) copy-start(f32[9,2,32,512]{3,2,1,0:T(8,128)} %param.12) | copy-start | bytes 3538948
  10.3 56.6 %copy-start.4 = (f32[9,512]{1,0:T(8,128)S(1)}, f32[9,512]{1,0:T(8,128)}, u32[]{:S(2)}) copy-start(f32[9,512]{1,0:T(8,128)} %param.15) | copy-start | bytes 55300
  65.2 1.6 %copy-start.1 = (f32[9,2,32,512]{3,2,1,0:T(8,128)S(1)}, f32[9,2,32,512]{3,2,1,0:T(8,128)}, u32[]{:S(2)}) copy-start(f32[9,2,32,512]{3,2,1,0:T(8,128)} %param.14) | copy-start | bytes 3538948
  65.3 2.0 %copy-start.2 = (f32[9,2,32,512]{3,2,1,0:T(8,128)S(1)}, f32[9,2,32,512]{3,2,1,0:T(8,128)}, u32[]{:S(2)}) copy-start(f32[9,2,32,512]{3,2,1,0:T(8,128)} %param.13) | copy-start | bytes 3538948

commit v2 on v1

v2 whole, which is shorter than its diff:
```python
import functools
import math

import jax
import jax.numpy as jnp
from jax import lax
from jax.experimental import pallas as pl
from jax.experimental.pallas import tpu as pltpu
from jax.sharding import PartitionSpec as P

COMP = 3
STOKES = 3
FIELDS = 9
BANDS = 9
LANES = 512
MESH = pl.DeviceIdType.MESH


def wave(phase, quarter):
    folded = jnp.abs(phase - 2 * quarter) - quarter
    x = folded.astype(jnp.float32) * (math.pi / (2 * quarter))
    x2 = x * x
    series = -1.0 / 39916800.0
    for coefficient in (1.0 / 362880.0, -1.0 / 5040.0, 1.0 / 120.0, -1.0 / 6.0, 1.0):
        series = series * x2 + coefficient
    return x * series


def wrapped(value, period):
    if period & (period - 1) == 0:
        return value & (period - 1)
    return lax.rem(value, period)


def contract(left, right, left_dim, right_dim):
    return lax.dot_general(
        left, right, (((left_dim,), (right_dim,)), ((), ())), preferred_element_type=jnp.float32
    )


def wait_bytes(ref, sem):
    pltpu.make_async_copy(ref, ref, sem).wait()


def kernel(
    sizes,
    direction,
    residual,
    precond,
    inv_spec,
    mixing,
    slot_band,
    m_order,
    cycle_order,
    beams,
    noise,
    mask,
    applied,
    step_row,
    ratio_row,
    tri,
    halved,
    colat,
    amps,
    send,
    recv,
    joint,
    turned,
    azim,
    side,
    back,
    back_send,
    back_recv,
    stats,
    send_sem,
    recv_sem,
    turn_send_sem,
    turn_recv_sem,
    back_send_sem,
    back_recv_sem,
    spread_send_sem,
    spread_recv_sem,
    stat_send_sem,
    stat_recv_sem,
):
    groups, blocks, slots, l_total, modes, phi_total = sizes
    rows, l_local = direction.shape[1:]
    cycle_total = cycle_order.shape[0]
    r_local = cycle_total // blocks
    pairs = slots * STOKES
    per_lane = 128 // rows
    my_band = lax.axis_index("band")
    my_block = lax.axis_index("blk")

    def target(step, shift):
        return (lax.rem(my_band + step, groups), lax.rem(my_block + shift, blocks))

    barrier = pltpu.get_barrier_semaphore()

    def greet(flat, carry):
        pl.semaphore_signal(
            barrier, inc=1, device_id=target(flat // blocks, flat % blocks), device_id_type=MESH
        )
        return carry

    lax.fori_loop(1, groups * blocks, greet, 0)

    def slot_row(at):
        band = slot_band[at]
        filled = jnp.where(band < BANDS, 1.0, 0.0)
        held = jnp.minimum(band, BANDS - 1)
        columns = pl.ds(pl.multiple_of(my_band * l_local, l_local), l_local)
        mix = [filled * mixing[comp, held] for comp in range(COMP)]
        return (mix, beams[pl.ds(held, 1), columns])

    def column(ref, first, count, width):
        place = lax.broadcasted_iota(jnp.int32, (8, 128), 0)
        pieces = []
        for at in range(0, count, 8):
            piece = jnp.full((8, 128), ref[first + at], jnp.int32)
            for inner in range(1, 8):
                piece = jnp.where(place == inner, ref[first + at + inner], piece)
            pieces.append(piece)
        tall = jnp.concatenate(pieces, axis=0)
        return jnp.concatenate([tall] * (width // 128), axis=1)

    l_index = my_band * l_local + lax.broadcasted_iota(jnp.int32, (1, l_local), 1)
    my_orders = column(m_order, my_block * (rows // 2), rows // 2, l_local)
    tri[...] = jnp.where(l_index >= jnp.concatenate([my_orders, my_orders], axis=0), 1.0, 0.0)
    for field in range(FIELDS):
        halved[field] = direction[field].astype(jnp.bfloat16).astype(jnp.float32) * tri[...]

    def colat_rows(at, carry):
        at_rows = pl.ds(pl.multiple_of(at * 64, 64), 64)
        phase = wrapped(l_index * (2 * column(cycle_order, at * 64, 64, l_local) + 1), 4 * cycle_total)
        colat[at_rows, :] = (wave(phase, cycle_total) / math.sqrt(l_total)).astype(jnp.bfloat16)
        return carry

    lax.fori_loop(0, cycle_total // 64, colat_rows, 0)

    def transform(step):
        group = lax.rem(my_band + step, groups)
        for slot in range(slots):
            at = group * slots + slot
            mix, beam = slot_row(at)
            for stokes in range(STOKES):
                mixed = mix[0] * halved[stokes]
                for comp in range(1, COMP):
                    mixed = mixed + mix[comp] * halved[comp * STOKES + stokes]
                first = (slot * STOKES + stokes) * rows
                amps[first : first + rows, :] = (mixed * beam).astype(jnp.bfloat16)
        send[step] = contract(colat[...], amps[...], 1, 1).astype(jnp.bfloat16)

    def block_rows(block):
        return pl.ds(pl.multiple_of(block * r_local, r_local), r_local)

    def ship(step):
        pltpu.make_async_remote_copy(
            src_ref=send.at[step],
            dst_ref=recv.at[step],
            send_sem=send_sem.at[step],
            recv_sem=recv_sem.at[step],
            device_id=target(step, 0),
            device_id_type=MESH,
        ).start()

    transform(1)
    pl.semaphore_wait(barrier, groups * blocks - 1)
    ship(1)

    def group_step(step, carry):
        transform(step)
        ship(step)
        return carry

    lax.fori_loop(2, groups, group_step, 0)
    transform(0)

    def fill_azim(chunk):
        cell = chunk * LANES + lax.broadcasted_iota(jnp.int32, (1, LANES), 1)

        def one(at, carry):
            at_rows = pl.ds(pl.multiple_of(at * 2 * rows, 2 * rows), 2 * rows)
            phases = []
            for inner in range(2):
                orders = column(m_order, (at * 2 + inner) * (rows // 2), rows // 2, LANES)
                phases += [orders * cell, orders * cell + phi_total // 4]
            phase = wrapped(jnp.concatenate(phases, axis=0), phi_total)
            azim[at_rows, :] = (wave(phase, phi_total // 4) / math.sqrt(modes)).astype(jnp.bfloat16)
            return carry

        lax.fori_loop(0, blocks // 2, one, 0)

    chunks = phi_total // LANES
    if chunks == 1:
        fill_azim(0)
    rest = (blocks - 1) * r_local
    for step in range(1, groups):
        wait_bytes(recv.at[step], recv_sem.at[step])

    def add_up(at, carry):
        at_rows = block_rows(at)
        total = send[0, at_rows, :].astype(jnp.float32)
        for step in range(1, groups):
            total = total + recv[step, at_rows, :].astype(jnp.float32)
        joint[at_rows, :] = total.astype(jnp.bfloat16)
        return carry

    lax.fori_loop(0, blocks, add_up, 0)

    def turn(shift, carry):
        there = target(0, shift)
        pltpu.make_async_remote_copy(
            src_ref=joint.at[block_rows(there[1])],
            dst_ref=turned.at[block_rows(shift)],
            send_sem=turn_send_sem,
            recv_sem=turn_recv_sem,
            device_id=there,
            device_id_type=MESH,
        ).start()
        return carry

    lax.fori_loop(1, blocks, turn, 0)
    turned[0:r_local] = joint[block_rows(my_block)]
    residual_sum = jnp.zeros((rows, l_local), jnp.float32)
    for field in range(FIELDS):
        residual_sum = residual_sum + residual[field] * (
            precond[field : field + 1] * residual[field]
        )
    wait_bytes(turned.at[r_local:cycle_total], turn_recv_sem)

    def gather(at, carry):
        parts = []
        for inner in range(per_lane):
            block = at * per_lane + inner
            rows_at = block_rows(lax.rem(my_block - block + blocks, blocks))
            parts.append(turned[rows_at, :].astype(jnp.float32))
        columns = pl.ds(pl.multiple_of(at * 128, 128), 128)
        for pair in range(pairs):
            picked = [part[:, pair * rows : (pair + 1) * rows] for part in parts]
            joined = jnp.concatenate(picked, axis=1).astype(jnp.bfloat16)
            side[pair * r_local : (pair + 1) * r_local, columns] = joined
        return carry

    lax.fori_loop(0, blocks // per_lane, gather, 0)

    def weigh(chunk):
        columns = pl.ds(pl.multiple_of(chunk * LANES, LANES), LANES)
        sky = contract(side[...], azim[...], 1, 0).reshape(pairs, r_local, LANES)
        weight = noise[:, :, columns] * mask[:, columns].astype(jnp.float32)[None]
        weighted = (weight * sky).astype(jnp.bfloat16).reshape(pairs * r_local, LANES)
        return contract(weighted, azim[...], 1, 1)

    if chunks == 1:
        back[...] = weigh(0)
    else:
        back[...] = jnp.zeros_like(back)

        def one_chunk(chunk, carry):
            fill_azim(chunk)
            back[...] += weigh(chunk)
            return carry

        lax.fori_loop(0, chunks, one_chunk, 0)

    def scatter(at, carry):
        columns = pl.ds(pl.multiple_of(at * 128, 128), 128)
        wide = [back[pair * r_local : (pair + 1) * r_local, columns] for pair in range(pairs)]
        for inner in range(per_lane):
            picked = [part[:, inner * rows : (inner + 1) * rows] for part in wide]
            joined = jnp.concatenate(picked, axis=1).astype(jnp.bfloat16)
            back_send[at * per_lane + inner] = joined
        return carry

    lax.fori_loop(0, blocks // per_lane, scatter, 0)

    def return_to(shift, carry):
        there = target(0, shift)
        pltpu.make_async_remote_copy(
            src_ref=back_send.at[there[1]],
            dst_ref=back_recv.at[0, block_rows(my_block)],
            send_sem=back_send_sem,
            recv_sem=back_recv_sem.at[shift],
            device_id=there,
            device_id_type=MESH,
        ).start()
        return carry

    def spread(block):
        for step in range(1, groups):
            pltpu.make_async_remote_copy(
                src_ref=back_recv.at[0, block_rows(block)],
                dst_ref=back_recv.at[step, block_rows(block)],
                send_sem=spread_send_sem.at[step],
                recv_sem=spread_recv_sem.at[step],
                device_id=target(step, 0),
                device_id_type=MESH,
            ).start()

    def pass_on(shift, carry):
        block = lax.rem(my_block - shift + blocks, blocks)
        arrived = back_recv.at[0, block_rows(block)]
        wait_bytes(arrived, back_recv_sem.at[shift])
        spread(block)
        return carry

    lax.fori_loop(1, blocks, return_to, 0)
    back_recv[0, block_rows(my_block)] = back_send[my_block]
    spread(my_block)
    lax.fori_loop(1, blocks, pass_on, 0)
    applied[...] = jnp.zeros_like(applied)

    def combine(step):
        group = lax.rem(my_band - step + groups, groups)
        harm = contract(back_recv[step], colat[...], 0, 0)
        held = [slot_row(group * slots + slot) for slot in range(slots)]
        for stokes in range(STOKES):
            sums = [applied[comp * STOKES + stokes] for comp in range(COMP)]
            for slot in range(slots):
                mix, beam = held[slot]
                first = (slot * STOKES + stokes) * rows
                term = harm[first : first + rows, :] * beam
                sums = [sums[comp] + mix[comp] * term for comp in range(COMP)]
            for comp in range(COMP):
                applied[comp * STOKES + stokes] = sums[comp]

    combine(0)

    def combine_step(step, carry):
        wait_bytes(back_recv.at[step], spread_recv_sem.at[step])
        combine(step)
        return carry

    lax.fori_loop(1, groups, combine_step, 0)

    curvature = jnp.zeros((rows, l_local), jnp.float32)
    crossed = jnp.zeros((rows, l_local), jnp.float32)
    squared = jnp.zeros((rows, l_local), jnp.float32)
    for field in range(FIELDS):
        held = direction[field]
        value = inv_spec[field : field + 1] * held + applied[field] * tri[...]
        applied[field] = value
        scaled = precond[field : field + 1] * value
        curvature = curvature + held * value
        crossed = crossed + residual[field] * scaled
        squared = squared + value * scaled

    def lane_sums(value):
        row = jnp.sum(value, axis=0, keepdims=True)
        return functools.reduce(
            jnp.add, [row[:, at : at + 128] for at in range(0, l_local, 128)]
        )

    stats[0] = jnp.concatenate(
        [lane_sums(v) for v in (residual_sum, curvature, crossed, squared)]
        + [jnp.zeros((4, 128), jnp.float32)],
        axis=0,
    )

    def tell(flat, carry):
        pltpu.make_async_remote_copy(
            src_ref=stats.at[0],
            dst_ref=stats.at[flat],
            send_sem=stat_send_sem,
            recv_sem=stat_recv_sem,
            device_id=target(flat // blocks, flat % blocks),
            device_id_type=MESH,
        ).start()
        return carry

    lax.fori_loop(1, groups * blocks, tell, 0)
    wait_bytes(stats.at[1 : groups * blocks], stat_recv_sem)
    summed = jnp.sum(jnp.sum(stats[...], axis=0), axis=1, keepdims=True)
    wide = [jnp.broadcast_to(summed[at : at + 1], (1, l_local)) for at in range(4)]
    step_size = wide[0] / wide[1]
    norm_new = wide[0] - 2.0 * step_size * wide[2] + step_size * step_size * wide[3]
    step_row[...] = step_size
    ratio_row[...] = norm_new / wide[0]

    wait_bytes(stats.at[1 : groups * blocks], stat_send_sem)
    wait_bytes(joint.at[0:rest], turn_send_sem)
    wait_bytes(joint.at[0:rest], back_send_sem)
    for step in range(1, groups):
        wait_bytes(send.at[step], send_sem.at[step])
        wait_bytes(back_recv.at[step], spread_send_sem.at[step])


def on_device(
    solution,
    residual,
    direction,
    precond,
    inv_spec,
    mixing,
    beams,
    slot_band,
    m_order,
    cycle_order,
    inv_noise,
    pix_mask,
):
    groups = lax.axis_size("band")
    blocks = lax.axis_size("blk")
    m_local, l_local = direction.shape[2:]
    rows = 2 * m_local
    modes = m_order.shape[0]
    cycle_total = cycle_order.shape[0]
    slots, _, r_local, phi_total = inv_noise.shape
    pairs = slots * STOKES
    devices = groups * blocks

    vmem = pl.BlockSpec(memory_space=pltpu.VMEM)
    smem = pl.BlockSpec(memory_space=pltpu.SMEM)
    bf16, f32 = jnp.bfloat16, jnp.float32
    field_shape = (FIELDS, rows, l_local)
    dma = pltpu.SemaphoreType.DMA
    sizes = (groups, blocks, slots, l_local * groups, modes, phi_total)
    applied, step_row, ratio_row = pl.pallas_call(
        functools.partial(kernel, sizes),
        out_shape=(
            jax.ShapeDtypeStruct(field_shape, f32),
            jax.ShapeDtypeStruct((1, l_local), f32),
            jax.ShapeDtypeStruct((1, l_local), f32),
        ),
        in_specs=[vmem] * 4 + [smem] * 4 + [vmem] * 3,
        out_specs=(vmem, vmem, vmem),
        scratch_shapes=[
            pltpu.VMEM((rows, l_local), f32),
            pltpu.VMEM(field_shape, f32),
            pltpu.VMEM((cycle_total, l_local), bf16),
            pltpu.VMEM((pairs * rows, l_local), bf16),
            pltpu.VMEM((groups, cycle_total, pairs * rows), bf16),
            pltpu.VMEM((groups, cycle_total, pairs * rows), bf16),
            pltpu.VMEM((cycle_total, pairs * rows), bf16),
            pltpu.VMEM((cycle_total, pairs * rows), bf16),
            pltpu.VMEM((blocks * rows, LANES), bf16),
            pltpu.VMEM((pairs * r_local, blocks * rows), bf16),
            pltpu.VMEM((pairs * r_local, blocks * rows), f32),
            pltpu.VMEM((blocks, r_local, pairs * rows), bf16),
            pltpu.VMEM((groups, cycle_total, pairs * rows), bf16),
            pltpu.VMEM((devices, 8, 128), f32),
            dma((groups,)),
            dma((groups,)),
            dma,
            dma,
            dma,
            dma((blocks,)),
            dma((groups,)),
            dma((groups,)),
            dma,
            dma,
        ],
        compiler_params=pltpu.CompilerParams(
            collective_id=0, has_side_effects=True, vmem_limit_bytes=60 * 1024 * 1024
        ),
    )(
        direction.reshape(field_shape),
        residual.reshape(field_shape),
        precond,
        inv_spec,
        mixing.T,
        slot_band,
        m_order,
        cycle_order,
        beams,
        inv_noise.reshape(pairs, r_local, phi_total),
        pix_mask,
    )
    applied = applied.reshape(direction.shape)
    step_size, ratio = (row[:, None, None, :] for row in (step_row, ratio_row))
    precond_full = precond[:, None, None, :]
    solution_next = solution + step_size * direction
    residual_next = residual - step_size * applied
    direction_next = precond_full * residual_next + ratio * direction
    return (solution_next, residual_next, direction_next)


def solution(mesh):
    field = P(None, None, "blk", "band")
    return jax.shard_map(
        on_device,
        mesh=mesh,
        in_specs=(
            field,
            field,
            field,
            P(None, "band"),
            P(None, "band"),
            P(),
            P(),
            P(),
            P(),
            P(),
            P("band", None, "blk", None),
            P("blk", None),
        ),
        out_specs=(field, field, field),
        check_vma=False,
    )
```

time: 69.9 us -> 47.6 us (0.68)
  local copies, waits for them, and re-layouts: 10.4 us -> 0.01 us
  Pallas kernels: 49.7 us -> 42.8 us
  between operations: 4.65 us -> 0.69 us
  other arithmetic: 4.77 us -> 3.87 us
    pallas_call x1, Pallas kernels: 49.7 us -> 42.8 us  [on_device(): pl.pallas_call(functools.partial(kernel, sizes), out_shape=(jax.ShapeDtyp...]
    broadcast_in_dim x4 -> x0, local copies, waits for them, and re-layouts: 4.76 us -> none  [the longest x1 1.39 us: on_device(): cycle_order[:, None]]
    reshape x5 -> x0, local copies, waits for them, and re-layouts: 3.08 us -> none  [the longest x1 0.9 us: on_device(): all_orders.reshape(blocks * rows, 1)]
    add x1, other arithmetic: 2.28 us -> 3.87 us  [on_device(): direction_next = precond_full * residual_next + ratio * direction]
    mul x1 -> x0, other arithmetic: 1.58 us -> none  [on_device(): residual_next = residual - step_size * applied]
    slice x1 -> x0, local copies, waits for them, and re-layouts: 1.36 us -> none  [on_device(): norm_old, curvature, crossed, squared = (totals[at, 0] for at in range(4))]
    unnamed x11 -> x6, local copies, waits for them, and re-layouts: 1.14 us -> 0.01 us
where the time goes in v2:
time: 47.6 us; the launch traced here: 47.4 us
  Pallas kernels  42.8 us (90%)
  other arithmetic  3.87 us (8%)
  between operations  0.69 us (1%)
    pallas_call x1, Pallas kernels, on_device(): pl.pallas_call(functools.partial(kernel, sizes), out_shape=(jax.ShapeDtyp...  42.8 us
    add x1, other arithmetic, on_device(): direction_next = precond_full * residual_next + ratio * direction  3.87 us

profile of v2, /device:TPU:0, one launch (start us, length us, event | category | flops | bytes accessed | tf_op | source)
XLA Modules:
  0.0 47.4 jit_solution(468916761853448035)
XLA Ops:
  0.6 0.0 copy-start
  0.6 0.0 copy-start.1
  0.7 0.0 copy-start.2
  0.7 42.8 %shard_map.139 = (f32[9,64,512]{2,1,0:T(8,128)}, f32[1,512]{1,0:T(1,128)}, f32[1,512]{1,0:T(1,128)}) custom-call(f32[9,64,512]{2,1,0:T(8,128)} %bitcast.7, f32[9,64,512]{2,1,0:T(8,128)} %bitcast.8, f32[9,512]{1,0:T(8,128)} %precond.1, f32[9,512]{1,0:T(8,128)} %inv_spec.1, f32[3,9]{1,0:T(4,128)} %bitcast.13, s32[12]{0:T(128)} %slot_band.1, s32[256]{0:T(256)} %m_order.1, ...), custom_call_target="tpu_custom_call" | custom-call | tf_op jit(solution)/shard_map/pallas_call | solution.py:418
  43.5 0.0 copy-done
  43.5 0.0 copy-done.1
  43.5 0.0 copy-done.2
  43.5 3.9 %multiply_add_fusion = (f32[9,2,32,512]{3,2,1,0:T(8,128)}, f32[9,2,32,512]{3,2,1,0:T(8,128)}, f32[9,2,32,512]{3,2,1,0:T(8,128)}) fusion(f32[9,2,32,512]{3,2,1,0:T(8,128)S(1)} %copy-done, f32[512]{0:T(512)} %bitcast.12, f32[9,512]{1,0:T(8,128)S(1)} %copy-done.2, f32[9,2,32,512]{3,2,1,0:T(8,128)S(1)} %copy-done.1, f32[9,2,32,512]{3,2,1,0:T(8,128)} %bitcast.9, ...), kind=kLoop, calls=%fused_computation | loop fusion | flops 2064384 | bytes 8280064 | tf_op jit(solution)/shard_map/add | solution.py:474
Async XLA Ops:
  0.6 42.9 %copy-start = (f32[9,2,32,512]{3,2,1,0:T(8,128)S(1)}, f32[9,2,32,512]{3,2,1,0:T(8,128)}, u32[]{:S(2)}) copy-start(f32[9,2,32,512]{3,2,1,0:T(8,128)} %param.14) | copy-start | bytes 3538948
  0.6 42.9 %copy-start.1 = (f32[9,2,32,512]{3,2,1,0:T(8,128)S(1)}, f32[9,2,32,512]{3,2,1,0:T(8,128)}, u32[]{:S(2)}) copy-start(f32[9,2,32,512]{3,2,1,0:T(8,128)} %param.13) | copy-start | bytes 3538948
  0.7 42.9 %copy-start.2 = (f32[9,512]{1,0:T(8,128)S(1)}, f32[9,512]{1,0:T(8,128)}, u32[]{:S(2)}) copy-start(f32[9,512]{1,0:T(8,128)} %precond.1) | copy-start | bytes 55300

commit v3 on v2

--- a/solution.py
+++ b/solution.py
@@ -45,7 +45,7 @@
 def kernel(
     sizes,
     direction,
-    residual,
+    residual_in,
     precond,
     inv_spec,
     mixing,
@@ -55,9 +55,11 @@
     beams,
     noise,
     mask,
-    applied,
+    applied_out,
     step_row,
     ratio_row,
+    residual,
+    applied,
     tri,
     halved,
     colat,
@@ -82,6 +84,7 @@
     spread_recv_sem,
     stat_send_sem,
     stat_recv_sem,
+    local_sem,
 ):
     groups, blocks, slots, l_total, modes, phi_total = sizes
     rows, l_local = direction.shape[1:]
@@ -92,8 +95,17 @@
     my_band = lax.axis_index("band")
     my_block = lax.axis_index("blk")
 
+    high, low, half = my_band // 2, my_band % 2, groups // 2
+
     def target(step, shift):
-        return (lax.rem(my_band + step, groups), lax.rem(my_block + shift, blocks))
+        band = (high + step // 2) % half * 2 + (low + step) % 2
+        return (band, lax.rem(my_block + shift, blocks))
+
+    def origin(step):
+        return (high - step // 2 + half) % half * 2 + (low + step) % 2
+
+    load = pltpu.make_async_copy(residual_in, residual, local_sem.at[0])
+    load.start()
 
     barrier = pltpu.get_barrier_semaphore()
 
@@ -139,7 +151,7 @@
     lax.fori_loop(0, cycle_total // 64, colat_rows, 0)
 
     def transform(step):
-        group = lax.rem(my_band + step, groups)
+        group = target(step, 0)[0]
         for slot in range(slots):
             at = group * slots + slot
             mix, beam = slot_row(at)
@@ -164,11 +176,12 @@
             device_id_type=MESH,
         ).start()
 
-    transform(1)
+    transform(groups - 1)
     pl.semaphore_wait(barrier, groups * blocks - 1)
-    ship(1)
-
-    def group_step(step, carry):
+    ship(groups - 1)
+
+    def group_step(at, carry):
+        step = groups - at
         transform(step)
         ship(step)
         return carry
@@ -222,6 +235,7 @@
 
     lax.fori_loop(1, blocks, turn, 0)
     turned[0:r_local] = joint[block_rows(my_block)]
+    load.wait()
     residual_sum = jnp.zeros((rows, l_local), jnp.float32)
     for field in range(FIELDS):
         residual_sum = residual_sum + residual[field] * (
@@ -286,8 +300,8 @@
         ).start()
         return carry
 
-    def spread(block):
-        for step in range(1, groups):
+    def spread(block, steps):
+        for step in steps:
             pltpu.make_async_remote_copy(
                 src_ref=back_recv.at[0, block_rows(block)],
                 dst_ref=back_recv.at[step, block_rows(block)],
@@ -301,17 +315,24 @@
         block = lax.rem(my_block - shift + blocks, blocks)
         arrived = back_recv.at[0, block_rows(block)]
         wait_bytes(arrived, back_recv_sem.at[shift])
-        spread(block)
-        return carry
+        spread(block, near)
+        return carry
+
+    def pass_far(block, carry):
+        spread(block, far)
+        return carry
+
+    near, far = range(1, groups - 1), range(groups - 1, groups)
 
     lax.fori_loop(1, blocks, return_to, 0)
     back_recv[0, block_rows(my_block)] = back_send[my_block]
-    spread(my_block)
+    spread(my_block, near)
     lax.fori_loop(1, blocks, pass_on, 0)
+    lax.fori_loop(0, blocks, pass_far, 0)
     applied[...] = jnp.zeros_like(applied)
 
     def combine(step):
-        group = lax.rem(my_band - step + groups, groups)
+        group = origin(step)
         harm = contract(back_recv[step], colat[...], 0, 0)
         held = [slot_row(group * slots + slot) for slot in range(slots)]
         for stokes in range(STOKES):
@@ -369,6 +390,8 @@
         return carry
 
     lax.fori_loop(1, groups * blocks, tell, 0)
+    store = pltpu.make_async_copy(applied, applied_out, local_sem.at[1])
+    store.start()
     wait_bytes(stats.at[1 : groups * blocks], stat_recv_sem)
     summed = jnp.sum(jnp.sum(stats[...], axis=0), axis=1, keepdims=True)
     wide = [jnp.broadcast_to(summed[at : at + 1], (1, l_local)) for at in range(4)]
@@ -377,6 +400,7 @@
     step_row[...] = step_size
     ratio_row[...] = norm_new / wide[0]
 
+    store.wait()
     wait_bytes(stats.at[1 : groups * blocks], stat_send_sem)
     wait_bytes(joint.at[0:rest], turn_send_sem)
     wait_bytes(joint.at[0:rest], back_send_sem)
@@ -410,6 +434,7 @@
     devices = groups * blocks
 
     vmem = pl.BlockSpec(memory_space=pltpu.VMEM)
+    whole = pl.BlockSpec(memory_space=pl.ANY)
     smem = pl.BlockSpec(memory_space=pltpu.SMEM)
     bf16, f32 = jnp.bfloat16, jnp.float32
     field_shape = (FIELDS, rows, l_local)
@@ -422,9 +447,11 @@
             jax.ShapeDtypeStruct((1, l_local), f32),
             jax.ShapeDtypeStruct((1, l_local), f32),
         ),
-        in_specs=[vmem] * 4 + [smem] * 4 + [vmem] * 3,
-        out_specs=(vmem, vmem, vmem),
+        in_specs=[vmem, whole, vmem, vmem] + [smem] * 4 + [vmem] * 3,
+        out_specs=(whole, vmem, vmem),
         scratch_shapes=[
+            pltpu.VMEM(field_shape, f32),
+            pltpu.VMEM(field_shape, f32),
             pltpu.VMEM((rows, l_local), f32),
             pltpu.VMEM(field_shape, f32),
             pltpu.VMEM((cycle_total, l_local), bf16),
@@ -449,6 +476,7 @@
             dma((groups,)),
             dma,
             dma,
+            dma((2,)),
         ],
         compiler_params=pltpu.CompilerParams(
             collective_id=0, has_side_effects=True, vmem_limit_bytes=60 * 1024 * 1024

time: 47.6 us -> 49 us (1.029)
  Pallas kernels: 42.8 us -> 44.2 us
    pallas_call x1, Pallas kernels: 42.8 us -> 44.2 us  [on_device(): pl.pallas_call(functools.partial(kernel, sizes), out_shape=(jax.ShapeDtyp...]
where the time goes in v3:
time: 49 us; the launch traced here: 48.8 us
  Pallas kernels  44.2 us (90%)
  other arithmetic  3.87 us (8%)
  between operations  0.69 us (1%)
    pallas_call x1, Pallas kernels, on_device(): pl.pallas_call(functools.partial(kernel, sizes), out_shape=(jax.ShapeDtyp...  44.2 us
    add x1, other arithmetic, on_device(): direction_next = precond_full * residual_next + ratio * direction  3.87 us

profile of v3, /device:TPU:0, one launch (start us, length us, event | category | flops | bytes accessed | tf_op | source)
XLA Modules:
  0.0 48.8 jit_solution(6290995947710521198)
XLA Ops:
  0.6 0.0 copy-start
  0.6 0.0 copy-start.1
  0.7 0.0 copy-start.2
  0.7 44.2 %shard_map.139 = (f32[9,64,512]{2,1,0:T(8,128)}, f32[1,512]{1,0:T(1,128)}, f32[1,512]{1,0:T(1,128)}) custom-call(f32[9,64,512]{2,1,0:T(8,128)} %bitcast.7, f32[9,64,512]{2,1,0:T(8,128)} %bitcast.8, f32[9,512]{1,0:T(8,128)} %precond.1, f32[9,512]{1,0:T(8,128)} %inv_spec.1, f32[3,9]{1,0:T(4,128)} %bitcast.13, s32[12]{0:T(128)} %slot_band.1, s32[256]{0:T(256)} %m_order.1, ...), custom_call_target="tpu_custom_call" | custom-call | tf_op jit(solution)/shard_map/pallas_call | solution.py:443
  44.9 0.0 copy-done
  44.9 0.0 copy-done.1
  44.9 0.0 copy-done.2
  44.9 3.9 %multiply_add_fusion = (f32[9,2,32,512]{3,2,1,0:T(8,128)}, f32[9,2,32,512]{3,2,1,0:T(8,128)}, f32[9,2,32,512]{3,2,1,0:T(8,128)}) fusion(f32[9,2,32,512]{3,2,1,0:T(8,128)S(1)} %copy-done, f32[512]{0:T(512)} %bitcast.12, f32[9,512]{1,0:T(8,128)S(1)} %copy-done.2, f32[9,2,32,512]{3,2,1,0:T(8,128)S(1)} %copy-done.1, f32[9,2,32,512]{3,2,1,0:T(8,128)} %bitcast.9, ...), kind=kLoop, calls=%fused_computation | loop fusion | flops 2064384 | bytes 8280064 | tf_op jit(solution)/shard_map/add | solution.py:502
Async XLA Ops:
  0.6 44.3 %copy-start = (f32[9,2,32,512]{3,2,1,0:T(8,128)S(1)}, f32[9,2,32,512]{3,2,1,0:T(8,128)}, u32[]{:S(2)}) copy-start(f32[9,2,32,512]{3,2,1,0:T(8,128)} %param.14) | copy-start | bytes 3538948
  0.6 44.3 %copy-start.1 = (f32[9,2,32,512]{3,2,1,0:T(8,128)S(1)}, f32[9,2,32,512]{3,2,1,0:T(8,128)}, u32[]{:S(2)}) copy-start(f32[9,2,32,512]{3,2,1,0:T(8,128)} %param.13) | copy-start | bytes 3538948
  0.7 44.3 %copy-start.2 = (f32[9,512]{1,0:T(8,128)S(1)}, f32[9,512]{1,0:T(8,128)}, u32[]{:S(2)}) copy-start(f32[9,512]{1,0:T(8,128)} %precond.1) | copy-start | bytes 55300
